TPU v7x, 128 devices: a whole 4x4x4 slice. The times are simulated.
128 devices in a mesh: seq: 8 (over x, core), span: 16 (over y, z).
Axes of the slice: x: 4, y: 4, z: 4, core: 2. Of those that a mesh axis runs over, the one named last changes fastest.
Arguments:
- llm_input: bfloat16 [1024, 5120], P(('seq', 'span')), may hold values from -6 to 6
- hidden_grad: bfloat16 [1024, 32768], P(None, ('seq', 'span')), may hold values from -1.5 to 1.5
- gate_act: bfloat16 [1024, 32768], P(None, ('seq', 'span')), may hold values from -6 to 6
- up_weight: bfloat16 [5120, 32768], P(None, ('seq', 'span')), may hold values from -0.078125 to 0.078125
- span_counts: int32 [32], replicated, may hold values from 16 to 48, as said below
- row_ticks: int32 [1024], replicated, may hold values from 0 to 47, as said below
- encoder_out: bfloat16 [16, 384, 1280], P('span'), may hold values from -6 to 6
- mlp_input: bfloat16 [16, 384, 1280], P('span'), may hold values from -6 to 6
- post_gain: float32 [1280], replicated, may hold values from 0.5 to 1.5
- post_bias: float32 [1280], replicated, may hold values from -3 to 3
- adapter_in: bfloat16 [5120, 5120], P(None, 'seq'), may hold values from -0.078125 to 0.078125
- adapter_out: bfloat16 [5120, 5120], P('seq'), may hold values from -0.078125 to 0.078125
- expand_weight: bfloat16 [1280, 5120], P(None, 'seq'), may hold values from -0.15625 to 0.15625
- expand_bias: float32 [5120], P('seq'), may hold values from -3 to 3
- contract_weight: bfloat16 [5120, 1280], P('seq'), may hold values from -0.078125 to 0.078125
Outputs:
- gate_act_grad: bfloat16 [1024, 32768], P(None, ('seq', 'span'))
- up_weight_grad: bfloat16 [5120, 32768], P(None, ('seq', 'span'))
- adapter_in_grad: bfloat16 [5120, 5120], P('span', 'seq')
- adapter_out_grad: bfloat16 [5120, 5120], P(('seq', 'span'))
- expand_weight_grad: bfloat16 [1280, 5120], P('span', 'seq')
- contract_weight_grad: bfloat16 [5120, 1280], P(('seq', 'span'))
- expand_bias_grad: float32 [5120], P('seq')
- post_gain_grad: float32 [1280], replicated
- post_bias_grad: float32 [1280], replicated
- contract_bias_grad: float32 [1280], replicated
- encoder_out_grad: bfloat16 [16, 384, 1280], P('span', 'seq')
- mlp_input_grad: bfloat16 [16, 384, 1280], P('span', 'seq')
Inputs may be any that keep to these rules, and one draw needn't show every extreme that they name: span_counts sums to 1024; its largest entry is exactly 48. `row_ticks`: the rows of each span are consecutive in the sequence, spans in order of their number, span k holding span_counts[k] rows; inside a span the tick rises by one from row to row.
All inputs are finite; a program needn't handle non-finite values.
Results may differ from a plain program's by a relative error of at most 0.03.
Values may be sent and summed in bfloat16 or wider, within the bound.
No kernel may reach another device: no remote copies, remote signals or barrier semaphores. Data moves between devices by JAX's collectives and lax.ppermute only.
A program may use at most 192 MiB of HBM per device.

v0:
```python
import math

import jax
import jax.numpy as jnp
from jax import lax
from jax.sharding import PartitionSpec as P

STACK = 4
CH_DEV = 2


EPSILON = 1e-05


def cut_along(shard, dim, size):
    before, after = (shard.shape[:dim], shard.shape[dim + 1 :])
    return jnp.moveaxis(shard.reshape(*before, size, -1, *after), dim, 0)


def sum_packed(arrays, axis, dims):
    size = lax.axis_size(axis)
    pieces = [cut_along(a, dim, size) for a, dim in zip(arrays, dims)]
    lines = jnp.concatenate([b.reshape(size, -1) for b in pieces], axis=1)
    extent = max(16, -(-lines.shape[1] // 1024) * 8)
    lines = jnp.pad(lines, ((0, 0), (0, extent * 128 - lines.shape[1]))).reshape(-1, 128)
    ravelled, at, finished = (lax.psum_scatter(lines, axis, tiled=True).reshape(-1), 0, [])
    for b in pieces:
        part = b[0]
        finished.append(ravelled[at : at + part.size].reshape(part.shape))
        at += part.size
    return tuple(finished)


def sent_and_summed(shard, axis, dim):
    size = lax.axis_size(axis)
    pieces = lax.all_to_all(cut_along(shard, dim, size), axis, 0, 0, tiled=True)
    return jnp.sum(pieces.astype(jnp.float32), axis=0)


def sent_to_all(shard, axis):
    copies = jnp.broadcast_to(shard, (lax.axis_size(axis), *shard.shape))
    return lax.all_to_all(copies, axis, split_axis=0, concat_axis=0, tiled=True)


def of_everyone(shard, axis):
    everything = sent_to_all(shard, axis)
    return jnp.sum(everything, axis=0)


def together(arrays, axis):
    ends = [0]
    for a in arrays:
        ends.append(ends[-1] + a.size)
    running = of_everyone(jnp.concatenate([a.ravel() for a in arrays]), axis)
    return tuple((running[b:e].reshape(a.shape) for a, b, e in zip(arrays, ends, ends[1:])))


def gelu_value(values):
    return 0.5 * values * (1.0 + lax.erf(values * (1.0 / math.sqrt(2.0))))


def gelu_slope(values):
    cumulative = 0.5 * (1.0 + lax.erf(values * (1.0 / math.sqrt(2.0))))
    return cumulative + values * jnp.exp(-0.5 * values * values) * (1.0 / math.sqrt(2.0 * math.pi))


def locate_rows(span_counts, row_ticks, capacity):
    span_ends = jnp.cumsum(span_counts)
    positions = jnp.arange(row_ticks.shape[0], dtype=jnp.int32)
    span_of = jnp.sum((positions[:, None] >= span_ends[None, :]).astype(jnp.int32), axis=1)
    return span_of * capacity + row_ticks


def contract_last(left, right):
    return lax.dot_general(
        left, right, (((1,), (1,)), ((), ())), preferred_element_type=jnp.float32
    )


def contract_first(left, right):
    return lax.dot_general(
        left, right, (((0,), (0,)), ((), ())), preferred_element_type=jnp.float32
    )


def per_device(
    llm_input,
    hidden_grad,
    gate_act,
    up_weight,
    span_counts,
    row_ticks,
    encoder_out,
    mlp_input,
    post_gain,
    post_bias,
    adapter_in,
    adapter_out,
    expand_weight,
    expand_bias,
    contract_weight,
):
    rows_all = row_ticks.shape[0]
    up_grad = (hidden_grad.astype(jnp.float32) * gate_act.astype(jnp.float32)).astype(jnp.bfloat16)
    frames_each = encoder_out.shape[1]
    width = encoder_out.shape[2]
    slots_each = frames_each // STACK
    capacity = slots_each // CH_DEV
    owner_count = lax.axis_size("span")
    slot_of = locate_rows(span_counts, row_ticks, capacity)
    total_slots = owner_count * slots_each
    matches = jnp.arange(total_slots, dtype=jnp.int32)[:, None] == slot_of[None, :]
    filled = jnp.any(matches, axis=1)
    source = jnp.sum(jnp.where(matches, jnp.arange(rows_all, dtype=jnp.int32)[None, :], 0), axis=1)
    picked = jnp.take(up_grad, source, axis=0) * filled[:, None].astype(jnp.bfloat16)
    partial_slots = lax.psum_scatter(
        contract_last(picked, up_weight).astype(jnp.bfloat16),
        "span",
        scatter_dimension=0,
        tiled=True,
    )
    token_grad = lax.psum(partial_slots, "seq")
    piece = lax.all_gather(llm_input, ("seq", "span"), axis=0, tiled=True)
    weight_sum = contract_first(piece, up_grad)
    block = jnp.dot(piece, up_weight, preferred_element_type=jnp.float32)
    up_rows = block
    weight_sum, up_rows = (weight_sum, up_rows)
    gate_act_grad = (hidden_grad.astype(jnp.float32) * up_rows).astype(jnp.bfloat16)
    up_weight_grad = weight_sum.astype(jnp.bfloat16)
    frames = encoder_out[0].astype(jnp.float32)
    centre = frames - jnp.mean(frames, axis=1, keepdims=True)
    rstd = lax.rsqrt(jnp.mean(centre * centre, axis=1, keepdims=True) + EPSILON)
    nhat = centre * rstd
    stacked = (nhat * post_gain + post_bias).reshape(slots_each, STACK * width).astype(jnp.bfloat16)
    pre_act = jnp.dot(stacked, adapter_in, preferred_element_type=jnp.float32)
    activity = gelu_value(pre_act).astype(jnp.bfloat16)
    act_grad = contract_last(token_grad, adapter_out)
    pre_grad = (act_grad * gelu_slope(pre_act)).astype(jnp.bfloat16)
    partial_out = contract_first(activity, token_grad)
    partial_in = contract_first(stacked, pre_grad)
    adapter_in_sum, adapter_out_sum = tuple(
        (
            part.astype(jnp.float32)
            for part in sum_packed(
                (partial_in.astype(jnp.bfloat16), partial_out.astype(jnp.bfloat16)), "span", (0, 0)
            )
        )
    )
    stacked_part = contract_last(pre_grad, adapter_in)
    mine_frames = frames_each // lax.axis_size("seq")
    seq_index = lax.axis_index("seq")
    normed_grad = (
        lax.psum(stacked_part.astype(jnp.bfloat16), "seq")
        .astype(jnp.float32)
        .reshape(frames_each, width)
    )
    scaled = normed_grad * post_gain
    resid = rstd * (
        scaled
        - jnp.mean(scaled, axis=1, keepdims=True)
        - nhat * jnp.mean(scaled * nhat, axis=1, keepdims=True)
    )
    resid = resid.astype(jnp.bfloat16)
    gain_part = jnp.sum(normed_grad * nhat, axis=0)
    shift_part = jnp.sum(normed_grad, axis=0)
    out_bias_part = jnp.sum(resid.astype(jnp.float32), axis=0)
    resid_mine = lax.dynamic_slice_in_dim(resid, seq_index * mine_frames, mine_frames, 0)
    inputs = mlp_input[0]
    hidden_pre = jnp.dot(inputs, expand_weight, preferred_element_type=jnp.float32) + expand_bias
    hidden_act = gelu_value(hidden_pre).astype(jnp.bfloat16)
    hidden_enc_grad = contract_last(resid, contract_weight)
    hidden_pre_grad = (hidden_enc_grad * gelu_slope(hidden_pre)).astype(jnp.bfloat16)
    partial_expand = contract_first(inputs, hidden_pre_grad)
    partial_contract = contract_first(hidden_act, resid)
    expand_sum, contract_sum = tuple(
        (
            part.astype(jnp.float32)
            for part in sum_packed(
                (partial_expand.astype(jnp.bfloat16), partial_contract.astype(jnp.bfloat16)),
                "span",
                (0, 0),
            )
        )
    )
    in_bias_part = jnp.sum(hidden_pre_grad.astype(jnp.float32), axis=0)
    mlp_part = contract_last(hidden_pre_grad, expand_weight)
    mlp_input_grad = sent_and_summed(mlp_part.astype(jnp.bfloat16), "seq", 0).astype(jnp.bfloat16)
    expand_bias_grad, post_gain_grad, post_bias_grad, contract_bias_grad = together(
        (in_bias_part, gain_part, shift_part, out_bias_part), "span"
    )
    return (
        gate_act_grad,
        up_weight_grad,
        adapter_in_sum.astype(jnp.bfloat16),
        adapter_out_sum.astype(jnp.bfloat16),
        expand_sum.astype(jnp.bfloat16),
        contract_sum.astype(jnp.bfloat16),
        expand_bias_grad,
        post_gain_grad,
        post_bias_grad,
        contract_bias_grad,
        resid_mine.reshape(1, mine_frames, width),
        mlp_input_grad.reshape(1, mine_frames, width),
    )


def solution(mesh):
    return jax.shard_map(
        per_device,
        mesh=mesh,
        in_specs=(
            P(("seq", "span"), None),
            P(None, ("seq", "span")),
            P(None, ("seq", "span")),
            P(None, ("seq", "span")),
            P(),
            P(),
            P("span", None, None),
            P("span", None, None),
            P(),
            P(),
            P(None, "seq"),
            P("seq", None),
            P(None, "seq"),
            P("seq"),
            P("seq", None),
        ),
        out_specs=(
            P(None, ("seq", "span")),
            P(None, ("seq", "span")),
            P("span", "seq"),
            P(("seq", "span"), None),
            P("span", "seq"),
            P(("seq", "span"), None),
            P("seq"),
            P(),
            P(),
            P(),
            P("span", "seq", None),
            P("span", "seq", None),
        ),
        check_vma=False,
    )
```

profile of v0, /device:TPU:1, one launch (start us, length us, event | category | flops | bytes accessed | tf_op | source)
XLA Modules:
  0.0 499.1 jit_solution(5520227393207789108)
XLA Ops:
  8.1 0.9 copy.35
  11.5 1.3 fusion.15
  12.8 5.4 %gather_fusion = bf16[1536,256]{1,0:T(8,128)(2,1)} fusion(bf16[1024,256]{1,0:T(8,128)(2,1)S(1)} %fusion.15, s32[2048]{0:T(1024)S(1)} %pad_clamp_fusion), kind=kCustom, calls=%fused_computation | custom fusion | bytes 1579008 | tf_op jit(solution)/shard_map/jit(_take)/gather | solution.py:115
  18.2 9.1 %convolution_convert_fusion = bf16[1536,5120]{1,0:T(8,128)(2,1)} fusion(bf16[5120,256]{1,0:T(8,128)(2,1)S(1)} %copy-done, bf16[1536,256]{1,0:T(8,128)(2,1)} %gather_fusion, pred[1536]{0:T(1024)(128)(4,1)S(1)} %compare_and_fusion, bf16[1536]{0:T(1024)(128)(2,1)S(1)} %convert_element_type.113), kind=kOutput, calls=%fused_computation.1 | convolution fusion | flops 4035182592 | bytes 19141120 | tf_op jit(solution)/shard_map/dot_general | solution.py:75
  27.4 2.7 reshape.176
  30.1 1.4 convert_reduce_fusion.2
  31.6 1.6 multiply_reduce_fusion
  33.6 1.6 copy.45
  35.6 1.6 copy.44
  37.3 98.7 %reduce-scatter.4.cloned.1.call-done = bf16[96,5120]{1,0:T(8,128)(2,1)} async-done(((bf16[1536,5120]{1,0:T(8,128)(2,1)}), bf16[96,5120]{1,0:T(8,128)(2,1)}) %reduce-scatter.4.cloned.1.call-update) | async-done | bytes 983056 | tf_op jit(solution)/shard_map/reduce_scatter | solution.py:116
  136.2 3.2 add_convert_fusion
  139.4 0.9 copy-done.2
  140.4 4.0 fusion.41
  144.4 53.9 %all-reduce.3.cloned.1.call-done = bf16[96,5120]{1,0:T(8,128)(2,1)} async-done(((bf16[96,5120]{1,0:T(8,128)(2,1)}), bf16[96,5120]{1,0:T(8,128)(2,1)}) %all-reduce.3.cloned.1.call-update) | async-done | bytes 983056 | tf_op jit(solution)/shard_map/psum | solution.py:122
  198.3 5.3 %fusion.14 = bf16[96,640]{1,0:T(8,128)(2,1)S(1)} fusion(bf16[96,5120]{1,0:T(8,128)(2,1)} %all-reduce.3.cloned.1.call-done, bf16[640,5120]{1,0:T(8,128)(2,1)} %param.26, f32[96,640]{1,0:T(8,128)S(1)} %fusion.41), kind=kOutput, calls=%fused_computation.41 | convolution fusion | flops 629760000 | bytes 7905280 | tf_op jit(solution)/shard_map/dot_general | solution.py:75
  203.6 5.9 %convolution_convert_fusion.4 = bf16[96,5120]{1,0:T(8,128)(2,1)} fusion(bf16[96,640]{1,0:T(8,128)(2,1)S(1)} %fusion.14, bf16[5120,640]{1,0:T(8,128)(2,1)} %param.25), kind=kOutput, calls=%fused_computation.10 | convolution fusion | flops 629637120 | bytes 7659520 | tf_op jit(solution)/shard_map/dot_general | solution.py:75
  209.5 2.5 reshape.168
  212.7 3.8 convolution_add_fusion
  216.4 4.6 convolution_convert_fusion.2
  221.0 6.8 %reshape_reshape.12 = bf16[16,204800]{1,0:T(8,128)(2,1)} reshape(bf16[5120,640]{1,0:T(8,128)(2,1)} %convolution_convert_fusion.2) | data formatting | bytes 13107200 | tf_op jit(solution)/shard_map/reshape;reshape | solution.py:23
  227.9 5.8 %convolution_convert_fusion.1 = bf16[640,5120]{1,0:T(8,128)(2,1)} fusion(bf16[96,5120]{1,0:T(8,128)(2,1)} %all-reduce.3.cloned.1.call-done, f32[96,640]{1,0:T(8,128)S(1)} %fusion.41), kind=kOutput, calls=%fused_computation.3 | convolution fusion | flops 632729600 | bytes 7782400 | tf_op jit(solution)/shard_map/dot_general | solution.py:81
  233.7 6.6 %reshape_reshape.13 = bf16[16,204800]{1,0:T(8,128)(2,1)} reshape(bf16[640,5120]{1,0:T(8,128)(2,1)} %convolution_convert_fusion.1) | data formatting | bytes 13107200 | tf_op jit(solution)/shard_map/reshape;reshape | solution.py:23
  240.3 38.6 %all-reduce.5.cloned.1.call-done = bf16[384,1280]{1,0:T(8,128)(2,1)} async-done(((bf16[384,1280]{1,0:T(8,128)(2,1)}), bf16[384,1280]{1,0:T(8,128)(2,1)}) %all-reduce.5.cloned.1.call-update) | async-done | bytes 983056 | tf_op jit(solution)/shard_map/psum | solution.py:153
  278.9 2.7 fusion.10
  283.8 1.0 convert_reduce_fusion.3
  285.7 2.2 fusion.2
  287.9 3.5 copy.36
  291.4 2.8 reshape_reshape.14
  294.2 3.7 convolution_convert_fusion.5
  297.9 2.8 reshape_reshape.15
  300.7 3.8 pad_maximum_fusion.1
  304.5 4.1 reshape.170
  308.7 14.0 %pad_maximum_fusion = bf16[16,409600]{1,0:T(8,128)(2,1)} fusion(bf16[16,204800]{1,0:T(8,128)(2,1)} %reshape_reshape.13, bf16[16,204800]{1,0:T(8,128)(2,1)} %reshape_reshape.12), kind=kLoop, calls=%fused_computation.2 | loop fusion | flops 26214400 | bytes 26214400 | tf_op jit(solution)/shard_map/concatenate | solution.py:23
  322.7 17.2 %reshape.165 = bf16[51200,128]{1,0:T(8,128)(2,1)} reshape(bf16[16,409600]{1,0:T(8,128)(2,1)} %pad_maximum_fusion) | data formatting | bytes 26214400 | tf_op jit(solution)/shard_map/reshape | solution.py:25
  340.0 8.0 %fusion.12 = bf16[1024,256]{1,0:T(8,128)(2,1)} fusion(bf16[1024,5120]{1,0:T(8,128)(2,1)} %all-gather.2.cloned.1.call-done, bf16[5120,256]{1,0:T(8,128)(2,1)S(1)} %copy-done, bf16[1024,256]{1,0:T(8,128)(2,1)} %param.16), kind=kOutput, calls=%fused_computation.38 | convolution fusion | flops 2685140992 | bytes 14155776 | tf_op jit(solution)/shard_map/dot_general | solution.py:125
  348.8 6.8 %all-to-all-start = ((f32[16,1,4480]{2,1,0:T(1,128)}), f32[16,1,4480]{2,1,0:T(1,128)S(1)}, u32[]{:S(2)}, u32[]{:S(2)}) async-start(f32[16,1,4480]{2,1,0:T(1,128)} %broadcast_in_dim.28), calls=%async_computation.3 | async-start | bytes 573440 | tf_op jit(solution)/shard_map/all_to_all | solution.py:42
  355.6 3.5 convolution_convert_fusion.7
  359.2 3.9 all-to-all-done
  363.1 9.4 %all-to-all-start.1 = ((bf16[8,48,1280]{2,1,0:T(8,128)(2,1)}), bf16[8,48,1280]{2,1,0:T(8,128)(2,1)}, u32[]{:S(2)}, u32[]{:S(2)}) async-start(bf16[8,48,1280]{2,1,0:T(8,128)(2,1)} %bitcast.56), calls=%async_computation.4 | async-start | bytes 1966080 | tf_op jit(solution)/shard_map/all_to_all | solution.py:36
  372.6 8.2 %fusion.1 = bf16[5120,256]{0,1:T(8,128)(2,1)} fusion(bf16[1024,256]{1,0:T(8,128)(2,1)S(1)} %fusion.15, bf16[1024,5120]{1,0:T(8,128)(2,1)} %all-gather.2.cloned.1.call-done), kind=kOutput, calls=%fused_computation.9 | convolution fusion | flops 2685665280 | bytes 13631488 | tf_op jit(solution)/shard_map/dot_general | solution.py:81
  380.8 4.4 copy.38
  385.2 1.6 dynamic-slice_bitcast_fusion
  388.1 2.0 reduce_sum.125
  390.1 1.0 fusion.39
  392.6 95.7 %reduce-scatter.6.cloned.1.call-done = bf16[3200,128]{1,0:T(8,128)(2,1)} async-done(((bf16[51200,128]{1,0:T(8,128)(2,1)}), bf16[3200,128]{1,0:T(8,128)(2,1)}) %reduce-scatter.6.cloned.1.call-update) | async-done | bytes 819216 | tf_op jit(solution)/shard_map/reduce_scatter | solution.py:26
  488.4 1.2 fusion.38
  489.5 1.1 reshape.166
  490.6 0.9 reshape.167
  (69 shorter events, 11.2 us)
Async XLA Ops:
  8.0 10.2 %copy-start = (bf16[5120,256]{1,0:T(8,128)(2,1)S(1)}, bf16[5120,256]{1,0:T(8,128)(2,1)}, u32[]{:S(2)}) copy-start(bf16[5120,256]{1,0:T(8,128)(2,1)} %param.18) | copy-start | bytes 7864324
  8.0 128.0 %reduce-scatter.4.cloned.1.call-start = ((), (), s32[]{:S(2)}) async-start(), calls=%async_computation.6 | async-start | bytes 16711680 | tf_op jit(solution)/shard_map/reduce_scatter | solution.py:116
  27.4 170.9 %all-reduce.3.cloned.1.call-start = ((), (), s32[]{:S(2)}) async-start(), calls=%async_computation.7 | async-start | bytes 1966080 | tf_op jit(solution)/shard_map/psum | solution.py:122
  35.6 1.7 copy-start.9
  35.6 1.7 copy-start.8
  136.0 142.9 %all-reduce.5.cloned.1.call-start = ((), (), s32[]{:S(2)}) async-start(), calls=%async_computation.9 | async-start | bytes 1966080 | tf_op jit(solution)/shard_map/psum | solution.py:153
  139.4 0.9 copy-start.2
  209.5 3.1 copy-start.11
  212.0 127.9 %all-gather.2.cloned.1.call-start = ((), (), s32[]{:S(2)}) async-start(), calls=%async_computation.5 | async-start | bytes 10567680 | tf_op jit(solution)/shard_map/all_gather | solution.py:123
  212.6 177.6 %reduce-scatter.8.cloned.1.call-start = ((), (), s32[]{:S(2)}) async-start(), calls=%async_computation.10 | async-start | bytes 3481600 | tf_op jit(solution)/shard_map/reduce_scatter | solution.py:26
  212.6 3.8 copy-start.3
  278.9 2.7 copy-start.1
  278.9 2.7 copy-start.4
  281.6 1.6 copy-start.10
  281.6 2.2 copy-start.12
  282.4 2.5 copy-start.5
  283.8 1.8 copy-start.6
  284.9 0.8 copy-start.7
  308.6 179.7 %reduce-scatter.6.cloned.1.call-start = ((), (), s32[]{:S(2)}) async-start(), calls=%async_computation.8 | async-start | bytes 13926400 | tf_op jit(solution)/shard_map/reduce_scatter | solution.py:26
  348.8 14.3 %all-to-all-start = ((f32[16,1,4480]{2,1,0:T(1,128)}), f32[16,1,4480]{2,1,0:T(1,128)S(1)}, u32[]{:S(2)}, u32[]{:S(2)}) async-start(f32[16,1,4480]{2,1,0:T(1,128)} %broadcast_in_dim.28), calls=%async_computation.3 | async-start | bytes 573440 | tf_op jit(solution)/shard_map/all_to_all | solution.py:42
  363.1 25.0 %all-to-all-start.1 = ((bf16[8,48,1280]{2,1,0:T(8,128)(2,1)}), bf16[8,48,1280]{2,1,0:T(8,128)(2,1)}, u32[]{:S(2)}, u32[]{:S(2)}) async-start(bf16[8,48,1280]{2,1,0:T(8,128)(2,1)} %bitcast.56), calls=%async_computation.4 | async-start | bytes 1966080 | tf_op jit(solution)/shard_map/all_to_all | solution.py:36
Sparse Core Ops, SparseCore 0:
  27.5 108.4 reduce-scatter.3
  138.4 59.8 all-reduce.2
  212.1 66.7 all-reduce.4
  308.8 79.8 reduce-scatter.7
  391.9 96.3 reduce-scatter.5
Sparse Core Ops, SparseCore 1:
  215.5 73.4 all-gather.1
where the time goes:
time: 506 us; the launch traced here: 499 us
  waiting for transfers between devices  292 us (58%)
  local copies, waits for them, and re-layouts  76.2 us (15%)
  matrix products  65.2 us (13%)
  other arithmetic  33.4 us (7%)
  starting transfers between devices  16.7 us (3%)
  between operations  16 us (3%)
    reduce_scatter x1, waiting for transfers between devices, per_device(): lax.psum_scatter(contract_last(picked, up_weight).astype(jnp.bfloat16), '...  98.7 us
    reduce_scatter x2, waiting for transfers between devices, sum_packed(): lax.psum_scatter(lines, axis, tiled=True).reshape(-1)  95.7 us
    psum x1, waiting for transfers between devices, per_device(): token_grad = lax.psum(partial_slots, 'seq')  53.9 us
    psum x1, waiting for transfers between devices, per_device(): lax.psum(stacked_part.astype(jnp.bfloat16), 'seq').astype(jnp.float32)  38.6 us
    dot_general x5, matrix products, contract_last(): lax.dot_general(left, right, (((1,), (1,)), ((), ())), preferred_element_...  24.9 us
    dot_general x5, matrix products, contract_first(): lax.dot_general(left, right, (((0,), (0,)), ((), ())), preferred_element_...  24.5 us
    reshape x2, local copies, waits for them, and re-layouts, sum_packed(): jnp.pad(lines, ((0, 0), (0, extent * 128 - lines.shape[1])))  21.3 us
    another operation x4, local copies, waits for them, and re-layouts, sum_packed(): lines = jnp.concatenate([b.reshape(size, -1) for b in pieces], axis=1)  19.1 us
  transfers between devices with their start and end apart: 8, of which 5 were waited for; matrix products, arithmetic and copies ran while one was open for 27% of the time, Pallas kernels for 0%

commit v1 on v0

v1 whole, which is shorter than its diff:
```python
import math

import jax
import jax.numpy as jnp
from jax import lax
from jax.experimental import pallas as pl
from jax.experimental.pallas import tpu as pltpu
from jax.sharding import PartitionSpec as P

STACK = 4
CH_DEV = 2


EPSILON = 1e-05


def exchanged(pieces, axis):
    return lax.all_to_all(pieces, axis, 0, 0, tiled=True)


def sent_and_summed(shard, axis):
    size = lax.axis_size(axis)
    pieces = exchanged(shard.reshape(size, shard.shape[0] // size, *shard.shape[1:]), axis)
    return jnp.sum(pieces.astype(jnp.float32), axis=0)


def of_everyone(shard, axis):
    copies = jnp.broadcast_to(shard, (lax.axis_size(axis), *shard.shape))
    return jnp.sum(exchanged(copies, axis), axis=0)


def gelu_value(values):
    return 0.5 * values * (1.0 + lax.erf(values * (1.0 / math.sqrt(2.0))))


def gelu_slope(values):
    cumulative = 0.5 * (1.0 + lax.erf(values * (1.0 / math.sqrt(2.0))))
    return cumulative + values * jnp.exp(-0.5 * values * values) * (1.0 / math.sqrt(2.0 * math.pi))


def locate_rows(span_counts, row_ticks, capacity):
    span_ends = jnp.cumsum(span_counts)
    positions = jnp.arange(row_ticks.shape[0], dtype=jnp.int32)
    span_of = jnp.sum((positions[:, None] >= span_ends[None, :]).astype(jnp.int32), axis=1)
    return span_of * capacity + row_ticks


def contract_last(left, right):
    return lax.dot_general(
        left, right, (((1,), (1,)), ((), ())), preferred_element_type=jnp.float32
    )


def contract_first(left, right):
    return lax.dot_general(
        left, right, (((0,), (0,)), ((), ())), preferred_element_type=jnp.float32
    )


def column_block_kernel(grad_ref, weight_ref, out_ref):
    out_ref[0] = contract_last(grad_ref[...], weight_ref[...]).astype(out_ref.dtype)


def column_blocks(grad, weight, blocks):
    rows, inner = grad.shape
    width = weight.shape[0] // blocks
    return pl.pallas_call(
        column_block_kernel,
        grid=(blocks,),
        in_specs=[
            pl.BlockSpec((rows, inner), lambda i: (0, 0)),
            pl.BlockSpec((width, inner), lambda i: (i, 0)),
        ],
        out_specs=pl.BlockSpec((1, rows, width), lambda i: (i, 0, 0)),
        out_shape=jax.ShapeDtypeStruct((blocks, rows, width), jnp.bfloat16),
        cost_estimate=pl.CostEstimate(
            flops=2 * rows * inner * width * blocks,
            bytes_accessed=2 * (rows * inner + blocks * width * (inner + rows)),
            transcendentals=0,
        ),
        name="column_blocks",
    )(grad, weight)


def normalized(frames):
    centre = frames - jnp.mean(frames, axis=1, keepdims=True)
    rstd = lax.rsqrt(jnp.mean(centre * centre, axis=1, keepdims=True) + EPSILON)
    return centre * rstd, rstd


def per_device(
    llm_input,
    hidden_grad,
    gate_act,
    up_weight,
    span_counts,
    row_ticks,
    encoder_out,
    mlp_input,
    post_gain,
    post_bias,
    adapter_in,
    adapter_out,
    expand_weight,
    expand_bias,
    contract_weight,
):
    rows_all = row_ticks.shape[0]
    seq_size = lax.axis_size("seq")
    owner_count = lax.axis_size("span")
    seq_index = lax.axis_index("seq")
    frames_each = encoder_out.shape[1]
    width = encoder_out.shape[2]
    slots_each = frames_each // STACK
    capacity = slots_each // CH_DEV
    total_slots = owner_count * slots_each
    mine_frames = frames_each // seq_size

    piece = lax.all_gather(llm_input, ("seq", "span"), axis=0, tiled=True)
    up_grad = (hidden_grad.astype(jnp.float32) * gate_act.astype(jnp.float32)).astype(jnp.bfloat16)
    blocks = column_blocks(up_grad, up_weight, seq_size)
    partial_rows = lax.psum_scatter(
        blocks.reshape(seq_size * rows_all, blocks.shape[2]),
        "seq",
        scatter_dimension=0,
        tiled=True,
    )

    slot_of = locate_rows(span_counts, row_ticks, capacity)
    matches = jnp.arange(total_slots, dtype=jnp.int32)[:, None] == slot_of[None, :]
    placing = matches.astype(jnp.bfloat16)
    nhat, _ = normalized(encoder_out[0].astype(jnp.float32))
    stacked = (nhat * post_gain + post_bias).reshape(slots_each, STACK * width).astype(jnp.bfloat16)
    pre_act = jnp.dot(stacked, adapter_in, preferred_element_type=jnp.float32)
    activity = gelu_value(pre_act).astype(jnp.bfloat16)
    act_slope = gelu_slope(pre_act)
    stacked_cols = exchanged(
        jnp.moveaxis(stacked.reshape(slots_each, owner_count, -1), 1, 0), "span"
    ).reshape(total_slots, -1)
    inputs = mlp_input[0]
    hidden_pre = jnp.dot(inputs, expand_weight, preferred_element_type=jnp.float32) + expand_bias
    hidden_act = gelu_value(hidden_pre).astype(jnp.bfloat16)
    hidden_slope = gelu_slope(hidden_pre)
    mine = lax.dynamic_slice_in_dim(encoder_out[0], seq_index * mine_frames, mine_frames, 0)
    nhat_mine, rstd_mine = normalized(mine.astype(jnp.float32))
    (
        partial_rows,
        placing,
        activity,
        act_slope,
        stacked_cols,
        hidden_act,
        hidden_slope,
        nhat_mine,
        rstd_mine,
    ) = lax.optimization_barrier(
        (
            partial_rows,
            placing,
            activity,
            act_slope,
            stacked_cols,
            hidden_act,
            hidden_slope,
            nhat_mine,
            rstd_mine,
        )
    )

    partial_slots = jnp.dot(placing, partial_rows, preferred_element_type=jnp.float32)
    partial_slots, piece = lax.optimization_barrier((partial_slots.astype(jnp.bfloat16), piece))
    owned = exchanged(partial_slots.reshape(owner_count, slots_each, -1), "span")
    up_rows = jnp.dot(piece, up_weight, preferred_element_type=jnp.float32)
    gate_act_grad = (hidden_grad.astype(jnp.float32) * up_rows).astype(jnp.bfloat16)
    up_weight_grad = contract_first(piece, up_grad).astype(jnp.bfloat16)
    owned, gate_act_grad, up_weight_grad = lax.optimization_barrier(
        (owned, gate_act_grad, up_weight_grad)
    )
    token_block = jnp.sum(owned.astype(jnp.float32), axis=0).astype(jnp.bfloat16)
    token_grad = lax.all_gather(token_block, "seq", axis=1, tiled=True)

    pre_grad = (contract_last(token_grad, adapter_out) * act_slope).astype(jnp.bfloat16)
    pre_grad_all = lax.all_gather(pre_grad, "span", axis=0, tiled=True)
    normed_part = contract_last(pre_grad, adapter_in).astype(jnp.bfloat16)
    normed_part, activity = lax.optimization_barrier((normed_part, activity))
    normed_grad = sent_and_summed(normed_part.reshape(frames_each, width), "seq")
    adapter_out_grad = lax.psum_scatter(
        contract_first(activity, token_grad).astype(jnp.bfloat16),
        "span",
        scatter_dimension=0,
        tiled=True,
    )

    scaled = normed_grad * post_gain
    resid_mine = rstd_mine * (
        scaled
        - jnp.mean(scaled, axis=1, keepdims=True)
        - nhat_mine * jnp.mean(scaled * nhat_mine, axis=1, keepdims=True)
    )
    resid_mine = resid_mine.astype(jnp.bfloat16)
    resid = lax.all_gather(resid_mine, "seq", axis=0, tiled=True)

    contract_part = contract_first(hidden_act, resid).astype(jnp.bfloat16)
    contract_part, resid = lax.optimization_barrier((contract_part, resid))
    contract_weight_grad = sent_and_summed(contract_part, "span").astype(jnp.bfloat16)
    hidden_pre_grad = (contract_last(resid, contract_weight) * hidden_slope).astype(jnp.bfloat16)
    expand_part = contract_first(inputs, hidden_pre_grad).astype(jnp.bfloat16)
    expand_part, hidden_pre_grad = lax.optimization_barrier((expand_part, hidden_pre_grad))
    expand_weight_grad = sent_and_summed(expand_part, "span").astype(jnp.bfloat16)
    mlp_part = contract_last(hidden_pre_grad, expand_weight).astype(jnp.bfloat16)
    mlp_part, hidden_pre_grad, stacked_cols, normed_grad = lax.optimization_barrier(
        (mlp_part, hidden_pre_grad, stacked_cols, normed_grad)
    )
    mlp_input_grad = sent_and_summed(mlp_part, "seq").astype(jnp.bfloat16)
    expand_bias_grad = of_everyone(jnp.sum(hidden_pre_grad.astype(jnp.float32), axis=0), "span")
    adapter_in_grad = contract_first(stacked_cols, pre_grad_all).astype(jnp.bfloat16)
    sums = lax.psum(
        jnp.stack(
            [
                jnp.sum(normed_grad * nhat_mine, axis=0),
                jnp.sum(normed_grad, axis=0),
                jnp.sum(resid_mine.astype(jnp.float32), axis=0),
            ]
        ),
        ("seq", "span"),
    )
    post_gain_grad, post_bias_grad, contract_bias_grad = sums[0], sums[1], sums[2]
    return (
        gate_act_grad,
        up_weight_grad,
        adapter_in_grad,
        adapter_out_grad,
        expand_weight_grad,
        contract_weight_grad,
        expand_bias_grad,
        post_gain_grad,
        post_bias_grad,
        contract_bias_grad,
        resid_mine.reshape(1, mine_frames, width),
        mlp_input_grad.reshape(1, mine_frames, width),
    )


def solution(mesh):
    return jax.shard_map(
        per_device,
        mesh=mesh,
        in_specs=(
            P(("seq", "span"), None),
            P(None, ("seq", "span")),
            P(None, ("seq", "span")),
            P(None, ("seq", "span")),
            P(),
            P(),
            P("span", None, None),
            P("span", None, None),
            P(),
            P(),
            P(None, "seq"),
            P("seq", None),
            P(None, "seq"),
            P("seq"),
            P("seq", None),
        ),
        out_specs=(
            P(None, ("seq", "span")),
            P(None, ("seq", "span")),
            P("span", "seq"),
            P(("seq", "span"), None),
            P("span", "seq"),
            P(("seq", "span"), None),
            P("seq"),
            P(),
            P(),
            P(),
            P("span", "seq", None),
            P("span", "seq", None),
        ),
        check_vma=False,
    )
```

time: 506 us -> 397 us (0.78); the launches traced: 499 us -> 396 us
  waiting for transfers between devices: 292 us -> 85.5 us
  blocking collectives: 0 us -> 173 us
  local copies, waits for them, and re-layouts: 76.2 us -> 16.2 us
  matrix products: 65.2 us -> 52.1 us
  other arithmetic: 33.4 us -> 20.6 us
  Pallas kernels: 0 us -> 9.4 us
  starting transfers between devices: 16.7 us -> 23.2 us
    reduce_scatter x3 -> x1, waiting for transfers between devices: 194 us -> 34.1 us  [per_device(): lax.psum_scatter(blocks.reshape(seq_size * rows_all, blocks.shape[2]), 's...]
    psum x2 -> x0, waiting for transfers between devices: 92.5 us -> none  [the longest x1 53.9 us: per_device(): token_grad = lax.psum(partial_slots, 'seq')]
    psum x0 -> x1, blocking collectives: none -> 82.4 us  [per_device(): lax.psum(jnp.stack([jnp.sum(normed_grad * nhat_mine, axis=0), jnp.sum(nor...]
    all_to_all x0 -> x3, blocking collectives: none -> 59.6 us  [exchanged(): return lax.all_to_all(pieces, axis, 0, 0, tiled=True)]
    all_gather x0 -> x2, blocking collectives: none -> 31.1 us  [the longest x1 16.2 us: per_device(): token_grad = lax.all_gather(token_block, 'seq', axis=1, tiled=True)]
    reshape x8 -> x0, local copies, waits for them, and re-layouts: 28.8 us -> none  [the longest x2 21.3 us: sum_packed(): jnp.pad(lines, ((0, 0), (0, extent * 128 - lines.shape[1])))]
    all_gather x1, waiting for transfers between devices: 0.03 us -> 23.8 us  [per_device(): piece = lax.all_gather(llm_input, ('seq', 'span'), axis=0, tiled=True)]
    all_to_all x2 -> x4, waiting for transfers between devices: 3.94 us -> 27 us  [exchanged(): return lax.all_to_all(pieces, axis, 0, 0, tiled=True)]
  transfers between devices with their start and end apart: 8 -> 8, of which waited for: 5 -> 4; matrix products, arithmetic and copies ran while one was open for 27% -> 19% of each run, Pallas kernels for 0% -> 0%
where the time goes in v1:
time: 397 us; the launch traced here: 396 us
  blocking collectives  173 us (44%)
  waiting for transfers between devices  85.5 us (22%)
  matrix products  52.1 us (13%)
  starting transfers between devices  23.2 us (6%)
  other arithmetic  20.6 us (5%)
  local copies, waits for them, and re-layouts  16.2 us (4%)
  between operations  16 us (4%)
  Pallas kernels  9.4 us (2%)
    psum x1, blocking collectives, per_device(): lax.psum(jnp.stack([jnp.sum(normed_grad * nhat_mine, axis=0), jnp.sum(nor...  82.4 us
    all_to_all x3, blocking collectives, exchanged(): return lax.all_to_all(pieces, axis, 0, 0, tiled=True)  59.6 us
    reduce_scatter x1, waiting for transfers between devices, per_device(): lax.psum_scatter(blocks.reshape(seq_size * rows_all, blocks.shape[2]), 's...  34.1 us
    all_to_all x4, waiting for transfers between devices, exchanged(): return lax.all_to_all(pieces, axis, 0, 0, tiled=True)  27 us
    all_gather x1, waiting for transfers between devices, per_device(): piece = lax.all_gather(llm_input, ('seq', 'span'), axis=0, tiled=True)  23.8 us
    all_to_all x4, starting transfers between devices, exchanged(): return lax.all_to_all(pieces, axis, 0, 0, tiled=True)  23 us
    all_gather x1, blocking collectives, per_device(): token_grad = lax.all_gather(token_block, 'seq', axis=1, tiled=True)  16.2 us
    dot_general x5, matrix products, contract_first(): lax.dot_general(left, right, (((0,), (0,)), ((), ())), preferred_element_...  16 us
  transfers between devices with their start and end apart: 8, of which 4 were waited for; matrix products, arithmetic and copies ran while one was open for 19% of the time, Pallas kernels for 0%

profile of v1, /device:TPU:1, one launch (start us, length us, event | category | flops | bytes accessed | tf_op | source)
XLA Modules:
  0.0 396.1 jit_solution(3627122466172183895)
XLA Ops:
  8.1 2.3 fusion.12.grad_ref
  10.3 9.4 %column_blocks.1 = bf16[8,1024,640]{2,1,0:T(8,128)(2,1)} custom-call(bf16[1024,256]{1,0:T(8,128)(2,1)} %fusion.12.grad_ref, bf16[5120,256]{1,0:T(8,128)(2,1)} %weight_ref.1), custom_call_target="tpu_custom_call" | custom-call | flops 2684354560 | bytes 13631488 | tf_op jit(solution)/shard_map/column_blocks/pallas_call | solution.py:67
  19.8 0.5 all-gather.3.cloned.1.call-update
  20.4 0.6 copy-done.1
  20.9 2.2 reshape.182
  24.4 3.8 fusion.10
  28.2 8.6 %all-to-all-start = ((bf16[16,96,320]{2,1,0:T(8,128)(2,1)}), bf16[16,96,320]{2,1,0:T(8,128)(2,1)}, u32[]{:S(2)}, u32[]{:S(2)}) async-start(bf16[16,96,320]{2,1,0:T(8,128)(2,1)} %fusion.10), calls=%async_computation.1 | async-start | bytes 2359296 | tf_op jit(solution)/shard_map/all_to_all | solution.py:18
  36.8 1.9 reshape.181
  39.0 1.6 copy.51
  41.0 1.6 copy.50
  43.5 3.2 fusion
  46.7 2.2 fusion.16
  49.0 1.0 copy-done.4
  50.0 4.6 %fusion.29 = (f32[96,640]{1,0:T(8,128)S(1)}, bf16[96,640]{1,0:T(8,128)(2,1)S(1)}) fusion(bf16[5120,640]{1,0:T(8,128)(2,1)} %param.25, f32[96,5120]{1,0:T(8,128)S(1)} %bitcast.70, f32[96,5120]{1,0:T(8,128)S(1)} %copy-done.2, f32[96,5120]{1,0:T(8,128)S(1)} %bitcast.71, f32[5120]{0:T(1024)S(1)} %add.90, f32[5120]{0:T(1024)S(1)} %mul.181), kind=kOutput, calls=%fused_computation.55 | convolution fusion | flops 632279040 | bytes 12861440 | tf_op jit(solution)/shard_map/dot_general | solution.py:134
  54.6 34.1 %reduce-scatter.5.cloned.1.call-done = bf16[1024,640]{1,0:T(8,128)(2,1)} async-done(((bf16[8192,640]{1,0:T(8,128)(2,1)}), bf16[1024,640]{1,0:T(8,128)(2,1)}) %reduce-scatter.5.cloned.1.call-update) | async-done | bytes 1310736 | tf_op jit(solution)/shard_map/reduce_scatter | solution.py:122
  88.7 6.1 %convolution_convert_fusion.3 = bf16[1536,640]{1,0:T(8,128)(2,1)} fusion(bf16[1536,1024]{1,0:T(8,128)(2,1)} %fusion, bf16[1024,640]{1,0:T(8,128)(2,1)} %reduce-scatter.5.cloned.1.call-done), kind=kOutput, calls=%fused_computation.5 | convolution fusion | flops 2014248960 | bytes 6422528 | tf_op jit(solution)/shard_map/dot_general | solution.py:170
  94.9 23.8 %all-gather.3.cloned.1.call-done = bf16[1024,5120]{1,0:T(8,128)(2,1)} async-done(((bf16[8,5120]{1,0:T(8,128)(2,1)}), bf16[1024,5120]{1,0:T(8,128)(2,1)}) %all-gather.3.cloned.1.call-update) | async-done | bytes 10485776 | tf_op jit(solution)/shard_map/all_gather | solution.py:119
  118.7 4.9 %all-to-all-start.1 = ((bf16[16,96,640]{2,1,0:T(8,128)(2,1)}), bf16[16,96,640]{2,1,0:T(8,128)(2,1)}, u32[]{:S(2)}, u32[]{:S(2)}) async-start(bf16[16,96,640]{2,1,0:T(8,128)(2,1)} %bitcast.75), calls=%async_computation.2 | async-start | bytes 3932160 | tf_op jit(solution)/shard_map/all_to_all | solution.py:18
  123.7 8.6 %fusion.8 = bf16[1024,256]{1,0:T(8,128)(2,1)} fusion(bf16[1024,5120]{1,0:T(8,128)(2,1)} %all-gather.3.cloned.1.call-done, bf16[5120,256]{1,0:T(8,128)(2,1)} %weight_ref.1, bf16[1024,256]{1,0:T(8,128)(2,1)} %param.16), kind=kOutput, calls=%fused_computation.25 | convolution fusion | flops 2685140992 | bytes 14155776 | tf_op jit(solution)/shard_map/dot_general | solution.py:173
  132.3 4.5 %convolution_convert_fusion.1 = bf16[5120,256]{1,0:T(8,128)(2,1)} fusion(bf16[1024,5120]{1,0:T(8,128)(2,1)S(1)} %copy-done.16, bf16[1024,256]{1,0:T(8,128)(2,1)S(1)} %copy-done.7), kind=kOutput, calls=%fused_computation.1 | convolution fusion | flops 2685665280 | bytes 13631488 | tf_op jit(solution)/shard_map/dot_general | solution.py:55
  136.8 14.8 %all-to-all-done.1 = bf16[16,96,640]{2,1,0:T(8,128)(2,1)} async-done(((bf16[16,96,640]{2,1,0:T(8,128)(2,1)}), bf16[16,96,640]{2,1,0:T(8,128)(2,1)}, u32[]{:S(2)}, u32[]{:S(2)}) %all-to-all-start.1) | async-done | bytes 1966112 | tf_op jit(solution)/shard_map/all_to_all | solution.py:18
  151.6 1.8 reduce_sum.170
  153.4 16.2 %all_gather.13 = bf16[96,5120]{1,0:T(8,128)(2,1)S(1)} all-gather(bf16[96,640]{1,0:T(8,128)(2,1)S(1)} %reduce_sum.170), channel_id=1, replica_groups=mesh['seq'=8,'span'=16] {'seq'}, dimensions={1}, use_global_device_ids=true | all-gather | bytes 1105920 | tf_op jit(solution)/shard_map/all_gather | solution.py:180
  169.6 5.6 %fusion.11 = bf16[96,640]{1,0:T(8,128)(2,1)} fusion(f32[96,640]{1,0:T(8,128)S(1)} %get-tuple-element.45, bf16[96,5120]{1,0:T(8,128)(2,1)S(1)} %all_gather.13, bf16[640,5120]{1,0:T(8,128)(2,1)} %param.26), kind=kOutput, calls=%fused_computation.30 | convolution fusion | flops 629268480 | bytes 7905280 | tf_op jit(solution)/shard_map/dot_general | solution.py:49
  175.3 6.0 %convolution_convert_fusion.2 = bf16[96,5120]{1,0:T(8,128)(2,1)} fusion(bf16[96,640]{1,0:T(8,128)(2,1)} %fusion.11, bf16[5120,640]{1,0:T(8,128)(2,1)} %param.25), kind=kOutput, calls=%fused_computation.4 | convolution fusion | flops 629637120 | bytes 7659520 | tf_op jit(solution)/shard_map/dot_general | solution.py:49
  181.3 4.6 %convolution_convert_fusion = bf16[640,5120]{1,0:T(8,128)(2,1)} fusion(bf16[96,640]{1,0:T(8,128)(2,1)S(1)} %get-tuple-element.54, bf16[96,5120]{1,0:T(8,128)(2,1)S(1)} %all_gather.13), kind=kOutput, calls=%fused_computation | convolution fusion | flops 632422400 | bytes 7659520 | tf_op jit(solution)/shard_map/dot_general | solution.py:55
  186.0 1.2 copy-done.5
  187.2 1.5 reshape_reshape.3
  188.7 18.0 %all_to_all.36 = bf16[8,48,1280]{2,1,0:T(8,128)(2,1)S(1)} all-to-all(bf16[8,48,1280]{2,1,0:T(8,128)(2,1)} %reshape_reshape.3), channel_id=1, replica_groups=mesh['seq'=8,'span'=16] {'seq'}, dimensions={0} | all-to-all | bytes 1966080 | tf_op jit(solution)/shard_map/all_to_all | solution.py:18
  207.1 14.8 %all_gather.14 = bf16[384,1280]{1,0:T(8,128)(2,1)S(1)} all-gather(bf16[48,1280]{1,0:T(8,128)(2,1)S(1)} %get-tuple-element.68), channel_id=1, replica_groups=mesh['seq'=8,'span'=16] {'seq'}, dimensions={0}, use_global_device_ids=true | all-gather | bytes 1105920 | tf_op jit(solution)/shard_map/all_gather | solution.py:201
  222.0 2.3 convolution_convert_fusion.5
  224.2 1.0 fusion.9
  225.4 1.0 fusion.1
  226.5 2.0 convolution_convert_fusion.6
  228.6 10.1 %all_to_all.37 = f32[16,1,640]{2,1,0:T(1,128)} all-to-all(f32[16,1,640]{2,1,0:T(1,128)S(1)} %broadcast_in_dim.2), channel_id=1, replica_groups=mesh['seq'=8,'span'=16] {'span'}, dimensions={0} | all-to-all | bytes 81920 | tf_op jit(solution)/shard_map/all_to_all | solution.py:18
  238.6 5.7 %all-to-all-start.6 = ((bf16[8,48,1280]{2,1,0:T(8,128)(2,1)}), bf16[8,48,1280]{2,1,0:T(8,128)(2,1)}, u32[]{:S(2)}, u32[]{:S(2)}) async-start(bf16[8,48,1280]{2,1,0:T(8,128)(2,1)} %bitcast.76), calls=%async_computation.7 | async-start | bytes 1966080 | tf_op jit(solution)/shard_map/all_to_all | solution.py:18
  244.4 2.2 copy.47
  246.6 12.2 %all-to-all-done.6 = bf16[8,48,1280]{2,1,0:T(8,128)(2,1)} async-done(((bf16[8,48,1280]{2,1,0:T(8,128)(2,1)}), bf16[8,48,1280]{2,1,0:T(8,128)(2,1)}, u32[]{:S(2)}, u32[]{:S(2)}) %all-to-all-start.6) | async-done | bytes 983072 | tf_op jit(solution)/shard_map/all_to_all | solution.py:18
  258.8 31.6 %all_to_all.38 = bf16[16,80,640]{2,1,0:T(8,128)(2,1)} all-to-all(bf16[16,80,640]{2,1,0:T(8,128)(2,1)} %bitcast.74), channel_id=1, replica_groups=mesh['seq'=8,'span'=16] {'span'}, dimensions={0} | all-to-all | bytes 3276800 | tf_op jit(solution)/shard_map/all_to_all | solution.py:18
  290.4 3.7 all-to-all-start.4
  294.1 1.0 multiply_reduce_fusion
  295.2 82.4 %psum.7 = f32[3,1280]{1,0:T(4,128)S(1)} all-reduce(f32[3,1280]{1,0:T(4,128)S(1)} %pad_maximum_fusion), channel_id=1, replica_groups=mesh['seq'=8,'span'=16] {'seq','span'}, use_global_device_ids=true, to_apply=%region_19.20 | all-reduce | flops 3840 | bytes 30720 | tf_op jit(solution)/shard_map/psum | solution.py:217
  377.6 0.6 slice_reduce_fusion
  378.2 1.4 reduce_sum.177
  379.7 2.0 reduce_sum.181
  381.7 2.3 reduce_sum.174
  384.0 0.9 reduce_sum.175
  384.9 3.6 convolution_convert_fusion.7
  (90 shorter events, 3.8 us)
Async XLA Ops:
  8.0 38.7 %copy-start = (bf16[1280,640]{1,0:T(8,128)(2,1)S(1)}, bf16[1280,640]{1,0:T(8,128)(2,1)}, u32[]{:S(2)}) copy-start(bf16[1280,640]{1,0:T(8,128)(2,1)} %param.27) | copy-start | bytes 4915204
  8.0 80.7 %reduce-scatter.5.cloned.1.call-start = ((), (), s32[]{:S(2)}) async-start(), calls=%async_computation.9 | async-start | bytes 11796480 | tf_op jit(solution)/shard_map/reduce_scatter | solution.py:122
  19.7 1.2 copy-start.1
  19.8 98.9 %all-gather.3.cloned.1.call-start = ((), (), s32[]{:S(2)}) async-start(), calls=%async_computation.10 | async-start | bytes 10567680 | tf_op jit(solution)/shard_map/all_gather | solution.py:119
  20.9 3.2 copy-start.13
  23.1 1.1 copy-start.12
  28.2 26.4 %all-to-all-start = ((bf16[16,96,320]{2,1,0:T(8,128)(2,1)}), bf16[16,96,320]{2,1,0:T(8,128)(2,1)}, u32[]{:S(2)}, u32[]{:S(2)}) async-start(bf16[16,96,320]{2,1,0:T(8,128)(2,1)} %fusion.10), calls=%async_computation.1 | async-start | bytes 2359296 | tf_op jit(solution)/shard_map/all_to_all | solution.py:18
  41.0 1.7 copy-start.15
  41.0 2.4 copy-start.14
  42.6 4.1 %copy-start.18 = (f32[640]{0:T(1024)S(1)}, f32[640]{0:T(1024)}, u32[]{:S(2)}) copy-start(f32[640]{0:T(1024)} %param.28) | copy-start | bytes 7684
  42.9 3.8 copy-start.8
  43.5 163.5 %copy-start.6 = (f32[48,1280]{1,0:T(8,128)}, f32[48,1280]{1,0:T(8,128)S(1)}, u32[]{:S(2)}) copy-start(f32[48,1280]{1,0:T(8,128)S(1)} %fusion.23) | copy-start | bytes 737284
  46.7 2.3 copy-start.2
  46.7 2.3 copy-start.3
  46.7 3.3 copy-start.4
  118.7 32.9 %all-to-all-start.1 = ((bf16[16,96,640]{2,1,0:T(8,128)(2,1)}), bf16[16,96,640]{2,1,0:T(8,128)(2,1)}, u32[]{:S(2)}, u32[]{:S(2)}) async-start(bf16[16,96,640]{2,1,0:T(8,128)(2,1)} %bitcast.75), calls=%async_computation.2 | async-start | bytes 3932160 | tf_op jit(solution)/shard_map/all_to_all | solution.py:18
  123.6 8.7 %copy-start.7 = (bf16[1024,256]{1,0:T(8,128)(2,1)S(1)}, bf16[1024,256]{1,0:T(8,128)(2,1)}, u32[]{:S(2)}) copy-start(bf16[1024,256]{1,0:T(8,128)(2,1)} %fusion.12.grad_ref) | copy-start | bytes 1572868
  123.6 261.3 %all-gather.5.cloned.1.call-start = ((), (), s32[]{:S(2)}) async-start(), calls=%async_computation.11 | async-start | bytes 2088960 | tf_op jit(solution)/shard_map/all_gather | solution.py:183
  123.7 8.6 %copy-start.16 = (bf16[1024,5120]{1,0:T(8,128)(2,1)S(1)}, bf16[1024,5120]{1,0:T(8,128)(2,1)}, u32[]{:S(2)}) copy-start(bf16[1024,5120]{1,0:T(8,128)(2,1)} %all-gather.3.cloned.1.call-done) | copy-start | bytes 31457284
  175.3 213.3 %reduce-scatter.7.cloned.1.call-start = ((), (), s32[]{:S(2)}) async-start(), calls=%async_computation.12 | async-start | bytes 6963200
  185.9 1.2 copy-start.5
  206.7 15.3 %copy-start.10 = (bf16[384,640]{1,0:T(8,128)(2,1)S(1)}, bf16[384,640]{1,0:T(8,128)(2,1)}, u32[]{:S(2)}) copy-start(bf16[384,640]{1,0:T(8,128)(2,1)} %get-tuple-element.42) | copy-start | bytes 1474564
  207.1 17.1 %copy-start.11 = (bf16[48,1280]{1,0:T(8,128)(2,1)}, bf16[48,1280]{1,0:T(8,128)(2,1)S(1)}, u32[]{:S(2)}) copy-start(bf16[48,1280]{1,0:T(8,128)(2,1)S(1)} %get-tuple-element.68) | copy-start | bytes 368644
  207.1 17.1 %copy-start.17 = (bf16[640,1280]{1,0:T(8,128)(2,1)S(1)}, bf16[640,1280]{1,0:T(8,128)(2,1)}, u32[]{:S(2)}) copy-start(bf16[640,1280]{1,0:T(8,128)(2,1)} %param.29) | copy-start | bytes 4915204
  207.1 17.1 %copy-start.19 = (f32[384,640]{1,0:T(8,128)S(1)}, f32[384,640]{1,0:T(8,128)}, u32[]{:S(2)}) copy-start(f32[384,640]{1,0:T(8,128)} %get-tuple-element.50) | copy-start | bytes 2949124
  224.2 1.2 copy-start.9
  238.6 20.1 %all-to-all-start.6 = ((bf16[8,48,1280]{2,1,0:T(8,128)(2,1)}), bf16[8,48,1280]{2,1,0:T(8,128)(2,1)}, u32[]{:S(2)}, u32[]{:S(2)}) async-start(bf16[8,48,1280]{2,1,0:T(8,128)(2,1)} %bitcast.76), calls=%async_computation.7 | async-start | bytes 1966080 | tf_op jit(solution)/shard_map/all_to_all | solution.py:18
  290.4 93.6 %all-to-all-start.4 = ((bf16[16,40,1280]{2,1,0:T(8,128)(2,1)}), bf16[16,40,1280]{2,1,0:T(8,128)(2,1)S(1)}, u32[]{:S(2)}, u32[]{:S(2)}) async-start(bf16[16,40,1280]{2,1,0:T(8,128)(2,1)} %bitcast.14), calls=%async_computation.5 | async-start | bytes 3276800 | tf_op jit(solution)/shard_map/all_to_all | solution.py:18
Sparse Core Ops, SparseCore 0:
  19.9 68.7 reduce-scatter.4
Sparse Core Ops, SparseCore 1:
  23.2 95.4 all-gather.2
  175.4 39.5 all-gather.4
  218.8 105.7 reduce-scatter.6
